TPU v7x, 32 devices: a whole 2x2x4 slice. The times are simulated.
32 devices in a mesh: dp: 8 (over z, y), mp: 4 (over x, core).
Axes of the slice: x: 2, y: 2, z: 4, core: 2. Of those that a mesh axis runs over, the one named last changes fastest.
Arguments:
- hidden_input: bfloat16 [8192, 24], P('dp'), may hold values from -6 to 6
- output_cotangent: bfloat16 [8192, 8192], P('dp', 'mp'), may hold values from -0.023925781 to 0.023925781
- master_weights: float32 [24, 8192], P('dp', 'mp'), may hold values from -6 to 6
- first_codes: int32 [24, 8192], P('dp', 'mp'), may hold values from 0 to 15
- second_codes: int32 [24, 8192], P('dp', 'mp'), may hold values from 0 to 15
- first_rows: float32 [24], P('dp'), may hold values from 0.001 to 0.03
- first_cols: float32 [8192], P('mp'), may hold values from 0.001 to 0.03
- second_rows: float32 [24], P('dp'), may hold values from 1e-05 to 0.001
- second_cols: float32 [8192], P('mp'), may hold values from 1e-05 to 0.001
- step_count: int32 [], replicated, may hold values from 1 to 9
Outputs:
- new_master: float32 [24, 8192], P('dp', 'mp')
- update_ratio: float32 [24, 8192], P('dp', 'mp')
- gathered_params: bfloat16 [24, 8192], P(None, 'mp')
- first_scaled: float32 [24, 8192], P('dp', 'mp')
- second_scaled: float32 [24, 8192], P('dp', 'mp')
- new_first_rows: float32 [24], P('dp')
- new_first_cols: float32 [8192], P('mp')
- new_second_rows: float32 [24], P('dp')
- new_second_cols: float32 [8192], P('mp')
All inputs are finite; a program needn't handle non-finite values.
Results may differ from a plain program's by a relative error of at most 0.001.
Values may be sent and summed in bfloat16 or wider, within the bound.
A program may use at most 64 MiB of HBM per device.

v0:
```python
import functools

import jax
import jax.numpy as jnp
from jax import lax
from jax.experimental import pallas as pl
from jax.experimental.pallas import tpu as pltpu
from jax.sharding import PartitionSpec as P

MESH = pl.DeviceIdType.MESH
F32 = jnp.float32


SUB = 8
LANES = 128


def kernel(
    ndp,
    nmp,
    loads_per_part,
    hidden_hbm,
    cot_hbm,
    master_hbm,
    code1_hbm,
    code2_hbm,
    cols1_hbm,
    cols2_hbm,
    rows1_hbm,
    rows2_hbm,
    step_hbm,
    master_out,
    ratio_out,
    params_out,
    scaled1_out,
    scaled2_out,
    rows_out,
    cols_out,
    hidden,
    cot,
    master,
    code1,
    code2,
    cols1,
    cols2,
    rows1,
    rows2,
    step_count,
    share,
    grads,
    square,
    squares,
    params,
    maxcol,
    maxcols,
    maxrow,
    maxrows,
    old1,
    old2,
    weights,
    in_sem,
    cot_sem,
    send_sem,
    recv_sem,
):
    dp = lax.axis_index("dp")
    mp = lax.axis_index("mp")
    ndev = ndp * nmp
    flat = dp * nmp + mp
    rows, ncols = master.shape
    parts = ncols // (SUB * LANES)
    deep = rows * SUB
    pieces = parts * loads_per_part
    width = ncols // pieces

    def loop(count, body):
        def step(i, carry):
            body(i)
            return carry

        lax.fori_loop(0, count, step, 0, unroll=count <= 32)

    loads = [
        pltpu.make_async_copy(src, dst, in_sem.at[i])
        for i, (src, dst) in enumerate(
            (
                (hidden_hbm, hidden),
                (code1_hbm, code1),
                (code2_hbm, code2),
                (cols1_hbm, cols1),
                (cols2_hbm, cols2),
                (master_hbm, master),
                (rows1_hbm, rows1),
                (rows2_hbm, rows2),
                (step_hbm, step_count),
            )
        )
    ]
    cot_loads = [
        pltpu.make_async_copy(
            cot_hbm.at[:, pl.ds(c * width, width)], cot.at[c], cot_sem.at[c]
        )
        for c in range(pieces)
    ]
    def peer(k):
        other = lax.rem(flat + k + 1, ndev)
        return {"dp": lax.div(other, nmp), "mp": lax.rem(other, nmp)}

    barrier = pltpu.get_barrier_semaphore()
    loop(
        ndev - 1,
        lambda k: pl.semaphore_signal(
            barrier, inc=1, device_id=peer(k), device_id_type=MESH
        ),
    )

    loads[0].start()
    for copy in cot_loads:
        copy.start()
    for copy in loads[1:]:
        copy.start()

    def send_share(p):
        def body(k):
            to = lax.rem(dp + k + 1, ndp)
            pltpu.make_async_remote_copy(
                src_ref=share.at[p, pl.ds(pl.multiple_of(to * deep, SUB), deep)],
                dst_ref=grads.at[k, pl.ds(p * deep, deep)],
                send_sem=send_sem.at[0],
                recv_sem=recv_sem.at[0],
                device_id={"dp": to},
                device_id_type=MESH,
            ).start()

        return body

    loads[0].wait()
    per_piece = width // LANES
    for c in range(pieces):
        cot_loads[c].wait()
        term = jnp.dot(hidden[...], cot[c], preferred_element_type=F32)
        p = c // loads_per_part
        for i in range(per_piece):
            sub = (c % loads_per_part) * per_piece + i
            share[p, pl.ds(sub, ndp * rows, stride=SUB), :] = term[
                :, i * LANES : (i + 1) * LANES
            ]
        if c == loads_per_part - 1:
            pl.semaphore_wait(barrier, ndev - 1)
        if c % loads_per_part == loads_per_part - 1:
            loop(ndp - 1, send_share(p))

    for copy in loads[1:]:
        copy.wait()

    def dense(value, ref):
        for b in range(ncols // LANES):
            at = (b // SUB) * deep + b % SUB
            ref[pl.ds(at, rows, stride=SUB), :] = value[:, b * LANES : (b + 1) * LANES]

    dense(code1[...].astype(F32), old1)
    dense(code2[...].astype(F32), old2)
    dense(master[...], weights)

    def scale(row_of, cols):
        tiles = []
        for p in range(parts):
            for r in range(rows):
                tiles.append(jnp.minimum(row_of(r), cols[p * SUB : (p + 1) * SUB]))
        return jnp.concatenate(tiles, axis=0)

    def tile(x, p, r):
        at = p * deep + r * SUB
        return x[at : at + SUB]

    level1 = (old1[...] - 7.5) / 7.5
    moment1 = 0.9 * (level1 * scale(lambda r: rows1[:, r : r + 1], cols1[...]))
    level2 = (old2[...] + 1.0) / 16.0
    moment2 = 0.95 * (level2 * level2 * scale(lambda r: rows2[:, r : r + 1], cols2[...]))
    steps = step_count[...].astype(F32)
    fix1 = 1.0 - jnp.exp(steps * jnp.log(F32(0.9)))
    fix2 = 1.0 - jnp.exp(steps * jnp.log(F32(0.95)))

    def wait_all(ref, count, which):
        blocks = ref.at[pl.ds(0, count)]
        pltpu.make_async_copy(blocks, blocks, which).wait()

    def fold(fn, first, ref, count):
        if count <= 32:
            for k in range(count):
                first = fn(first, ref[k])
            return first
        return lax.fori_loop(0, count, lambda k, x: fn(x, ref[k]), first)

    mine = pl.ds(pl.multiple_of(dp * deep, SUB), deep)
    gradient = jnp.concatenate([share[p, mine, :] for p in range(parts)], axis=0)
    wait_all(grads, ndp - 1, recv_sem.at[0])
    gradient = fold(jnp.add, gradient, grads, ndp - 1)

    lanes = jnp.sum(gradient * gradient, axis=0, keepdims=True)
    square[0] = lanes

    def send_square(k):
        pltpu.make_async_remote_copy(
            src_ref=square.at[0],
            dst_ref=squares.at[ndev - 2 - k],
            send_sem=send_sem.at[1],
            recv_sem=recv_sem.at[1],
            device_id=peer(ndev - 2 - k),
            device_id_type=MESH,
        ).start()

    loop(ndev - 1, send_square)
    wait_all(squares, ndev - 1, recv_sem.at[1])
    lanes = lanes + jnp.sum(squares[...], axis=0)
    norm = jnp.sqrt(jnp.sum(lanes, axis=1, keepdims=True))
    entries = rows * ncols * ndev
    clipf = jnp.minimum(1.0, 0.01 * jnp.sqrt(F32(entries)) / (norm + 1e-6))
    clipped = clipf * gradient

    new1 = moment1 + 0.1 * clipped
    new2 = moment2 + 0.05 * (clipped * clipped)
    abs1 = jnp.abs(new1)

    def over_rows(x):
        tops = []
        for p in range(parts):
            top = tile(x, p, 0)
            for r in range(1, rows):
                top = jnp.maximum(top, tile(x, p, r))
            tops.append(top)
        return jnp.concatenate(tops, axis=0)

    maxcol[0, 0] = over_rows(abs1)
    maxcol[0, 1] = over_rows(new2)

    pair = pltpu.make_async_remote_copy(
        src_ref=maxcol.at[0],
        dst_ref=maxcol.at[1],
        send_sem=send_sem.at[5],
        recv_sem=recv_sem.at[5],
        device_id={"dp": dp + 1 - 2 * lax.rem(dp, 2)},
        device_id_type=MESH,
    )
    pair.start()

    def over_cols(x):
        tops = []
        for r in range(rows):
            top = tile(x, 0, r)
            for p in range(1, parts):
                top = jnp.maximum(top, tile(x, p, r))
            tops.append(jnp.max(top, axis=0, keepdims=True))
        return tops

    tops = jnp.concatenate(over_cols(abs1) + over_cols(new2), axis=0)
    maxrow[0] = jnp.broadcast_to(jnp.max(tops, axis=1, keepdims=True), tops.shape)

    def send_rows(k):
        pltpu.make_async_remote_copy(
            src_ref=maxrow.at[0],
            dst_ref=maxrows.at[k],
            send_sem=send_sem.at[3],
            recv_sem=recv_sem.at[3],
            device_id={"mp": lax.rem(mp + k + 1, nmp)},
            device_id_type=MESH,
        ).start()

    loop(nmp - 1, send_rows)

    ratio = new1 / fix1 / (jnp.sqrt(new2 / fix2) + 1e-8)
    old_weights = weights[...]
    new_weights = old_weights - 0.001 * (ratio + 0.1 * old_weights)
    params[dp] = new_weights.astype(jnp.bfloat16)

    def send_params(k):
        pltpu.make_async_remote_copy(
            src_ref=params.at[dp],
            dst_ref=params.at[dp],
            send_sem=send_sem.at[4],
            recv_sem=recv_sem.at[4],
            device_id={"dp": lax.rem(dp + k + 1, ndp)},
            device_id_type=MESH,
        ).start()

    loop(ndp - 1, send_params)


    def send_cols(k):
        pltpu.make_async_remote_copy(
            src_ref=maxcol.at[2],
            dst_ref=maxcols.at[k],
            send_sem=send_sem.at[2],
            recv_sem=recv_sem.at[2],
            device_id={"dp": lax.rem(dp + 2 * (k + 1), ndp)},
            device_id_type=MESH,
        ).start()

    pair.wait_recv()
    maxcol[2] = jnp.maximum(maxcol[0], maxcol[1])
    loop(ndp // 2 - 1, send_cols)
    master_out[...] = new_weights
    ratio_out[...] = ratio

    wait_all(maxrows, nmp - 1, recv_sem.at[3])
    toprow = fold(jnp.maximum, maxrow[0], maxrows, nmp - 1)
    rows_out[...] = toprow
    wait_all(maxcols, ndp // 2 - 1, recv_sem.at[2])
    topcol = fold(jnp.maximum, maxcol[2], maxcols, ndp // 2 - 1)
    cols_out[...] = topcol
    scaled1_out[...] = new1 / (scale(lambda r: toprow[r : r + 1], topcol[0]) + 1e-8)
    scaled2_out[...] = new2 / (
        scale(lambda r: toprow[rows + r : rows + r + 1], topcol[1]) + 1e-8
    )

    wait_all(params, ndp - 1, recv_sem.at[4])
    params_out[...] = params[...]

    wait_all(grads, ndp - 1, send_sem.at[0])
    wait_all(squares, ndev - 1, send_sem.at[1])
    pair.wait_send()
    wait_all(maxcols, ndp // 2 - 1, send_sem.at[2])
    wait_all(maxrows, nmp - 1, send_sem.at[3])
    wait_all(params, ndp - 1, send_sem.at[4])


def unpack(
    master,
    ratio,
    params,
    scaled1,
    scaled2,
    toprows,
    topcols,
    master_out,
    ratio_out,
    params_out,
    scaled1_out,
    scaled2_out,
    rows1_out,
    cols1_out,
    rows2_out,
    cols2_out,
    wide,
):
    rows, ncols = master_out.shape
    ndp = params.shape[0]
    parts = ncols // (SUB * LANES)
    deep = rows * SUB

    cols1_out[...] = topcols[0]
    cols2_out[...] = topcols[1]
    for r in range(rows):
        rows1_out[r] = jnp.max(toprows[r : r + 1, :])
        rows2_out[r] = jnp.max(toprows[rows + r : rows + r + 1, :])
    for j in range(ndp):
        block = params[j].astype(F32)
        for p in range(parts):
            wide[p, j * deep : (j + 1) * deep] = block[p * deep : (p + 1) * deep]
    for b in range(ncols // LANES):
        p, sub = b // SUB, b % SUB
        cols = slice(b * LANES, (b + 1) * LANES)
        part = pl.ds(p * deep + sub, rows, stride=SUB)
        master_out[:, cols] = master[part, :]
        ratio_out[:, cols] = ratio[part, :]
        scaled1_out[:, cols] = scaled1[part, :]
        scaled2_out[:, cols] = scaled2[part, :]
        params_out[:, cols] = wide[p, pl.ds(sub, ndp * rows, stride=SUB), :].astype(
            jnp.bfloat16
        )


def shards(
    ndp,
    nmp,
    hidden_input,
    output_cotangent,
    master_weights,
    first_codes,
    second_codes,
    first_rows,
    first_cols,
    second_rows,
    second_cols,
    step_count,
):
    rows, ncols = master_weights.shape
    tokens, width = hidden_input.shape
    parts = ncols // (SUB * LANES)
    loads = 2
    height = parts * rows * SUB
    hbm = pl.BlockSpec(memory_space=pltpu.HBM)
    smem = pl.BlockSpec(memory_space=pltpu.SMEM)
    vmem = pl.BlockSpec(memory_space=pltpu.VMEM)
    whole = jax.ShapeDtypeStruct((rows, ncols), F32)
    block = (height, LANES)
    line = (parts * SUB, LANES)
    dense = pltpu.VMEM(block, F32)
    results = pl.pallas_call(
        functools.partial(kernel, ndp, nmp, loads),
        out_shape=(
            dense,
            dense,
            pltpu.VMEM((ndp, *block), jnp.bfloat16),
            dense,
            dense,
            pltpu.VMEM((2 * rows, LANES), F32),
            pltpu.VMEM((2, *line), F32),
        ),
        in_specs=[hbm] * 10,
        out_specs=[vmem] * 7,
        scratch_shapes=[
            pltpu.VMEM((width, tokens), jnp.bfloat16),
            pltpu.VMEM((parts * loads, tokens, ncols // (parts * loads)), jnp.bfloat16),
            pltpu.VMEM((rows, ncols), F32),
            pltpu.VMEM((rows, ncols), jnp.int32),
            pltpu.VMEM((rows, ncols), jnp.int32),
            pltpu.VMEM(line, F32),
            pltpu.VMEM(line, F32),
            pltpu.VMEM((1, rows), F32),
            pltpu.VMEM((1, rows), F32),
            pltpu.VMEM((1, 1), jnp.int32),
            pltpu.VMEM((parts, ndp * rows * SUB, LANES), F32),
            pltpu.VMEM((ndp - 1, *block), F32),
            pltpu.VMEM((1, 1, LANES), F32),
            pltpu.VMEM((ndp * nmp - 1, 1, LANES), F32),
            pltpu.VMEM((ndp, *block), jnp.bfloat16),
            pltpu.VMEM((3, 2, *line), F32),
            pltpu.VMEM((ndp // 2 - 1, 2, *line), F32),
            pltpu.VMEM((1, 2 * rows, LANES), F32),
            pltpu.VMEM((nmp - 1, 2 * rows, LANES), F32),
            pltpu.VMEM(block, F32),
            pltpu.VMEM(block, F32),
            pltpu.VMEM(block, F32),
            pltpu.SemaphoreType.DMA((9,)),
            pltpu.SemaphoreType.DMA((parts * loads,)),
            pltpu.SemaphoreType.DMA((6,)),
            pltpu.SemaphoreType.DMA((6,)),
        ],
        compiler_params=pltpu.CompilerParams(
            collective_id=0, has_side_effects=True, vmem_limit_bytes=60 * 1024 * 1024
        ),
    )(
        hidden_input.T,
        output_cotangent,
        master_weights,
        first_codes,
        second_codes,
        first_cols.reshape(line),
        second_cols.reshape(line),
        first_rows.reshape(1, rows),
        second_rows.reshape(1, rows),
        step_count.reshape(1, 1),
    )
    scales = jax.ShapeDtypeStruct((rows,), F32)
    cols = jax.ShapeDtypeStruct(line, F32)
    outs = pl.pallas_call(
        unpack,
        out_shape=(
            whole,
            whole,
            jax.ShapeDtypeStruct((ndp * rows, ncols), jnp.bfloat16),
            whole,
            whole,
            scales,
            cols,
            scales,
            cols,
        ),
        in_specs=[vmem] * 7,
        out_specs=[vmem] * 5 + [smem, vmem] * 2,
        scratch_shapes=[pltpu.VMEM((parts, ndp * rows * SUB, LANES), F32)],
        compiler_params=pltpu.CompilerParams(vmem_limit_bytes=40 * 1024 * 1024),
    )(*results)
    return (*outs[:6], outs[6].reshape(ncols), outs[7], outs[8].reshape(ncols))


def solution(mesh):
    return jax.shard_map(
        functools.partial(shards, mesh.shape["dp"], mesh.shape["mp"]),
        mesh=mesh,
        in_specs=(
            P("dp", None),
            P("dp", "mp"),
            P("dp", "mp"),
            P("dp", "mp"),
            P("dp", "mp"),
            P("dp"),
            P("mp"),
            P("dp"),
            P("mp"),
            P(),
        ),
        out_specs=(
            P("dp", "mp"),
            P("dp", "mp"),
            P(None, "mp"),
            P("dp", "mp"),
            P("dp", "mp"),
            P("dp"),
            P("mp"),
            P("dp"),
            P("mp"),
        ),
        check_vma=False,
    )
```

profile of v0, /device:TPU:0, one launch (start us, length us, event | category | flops | bytes accessed | tf_op | source)
XLA Modules:
  0.0 25.4 jit_solution(2566520712415103571)
XLA Ops:
  1.3 23.3 %shard_map.169 = (f32[48,128]{1,0:T(8,128)S(1)}, f32[48,128]{1,0:T(8,128)S(1)}, bf16[8,48,128]{2,1,0:T(8,128)(2,1)S(1)}, f32[48,128]{1,0:T(8,128)S(1)}, f32[48,1...) custom-call(bf16[24,1024]{1,0:T(8,128)(2,1)} %bitcast.9, bf16[1024,2048]{1,0:T(8,128)(2,1)} %cot_hbm.1, ...), custom_call_target="tpu_custom_call" | custom-call | tf_op jit(solution)/shard_map/pallas_call | solution.py:399
  24.6 0.8 %shard_map.170 = (f32[3,2048]{1,0:T(4,128)}, f32[3,2048]{1,0:T(4,128)}, bf16[24,2048]{1,0:T(8,128)(2,1)}, f32[3,2048]{1,0:T(4,128)}, f32[3,2048]{1,0:T(4,128)}, ...) custom-call(f32[48,128]{1,0:T(8,128)S(1)} %get-tuple-element.25.master, ...), custom_call_target="tpu_custom_call" | custom-call | tf_op jit(solution)/shard_map/pallas_call | solution.py:457
where the time goes:
time: 25.5 us; the launch traced here: 25.4 us
  Pallas kernels  24.1 us (95%)
  between operations  1.3 us (5%)
    pallas_call x1, Pallas kernels, shards(): pl.pallas_call(functools.partial(kernel, ndp, nmp, loads), out_shape=(den...  23.3 us
    pallas_call x1, Pallas kernels, shards(): pl.pallas_call(unpack, out_shape=(whole, whole, jax.ShapeDtypeStruct((ndp...  0.76 us

commit v1 on v0

--- a/solution.py
+++ b/solution.py
@@ -9,6 +9,8 @@
 
 MESH = pl.DeviceIdType.MESH
 F32 = jnp.float32
+I16 = jnp.int16
+FULL = 32767.0
 
 
 SUB = 8
@@ -41,23 +43,28 @@
     master,
     code1,
     code2,
-    cols1,
-    cols2,
     rows1,
     rows2,
     step_count,
     share,
     grads,
-    square,
     squares,
-    params,
-    maxcol,
-    maxcols,
-    maxrow,
-    maxrows,
+    packs,
+    metas,
+    mcodes,
+    mcols,
+    gq,
+    gscale,
+    gm,
+    gmscale,
     old1,
     old2,
     weights,
+    all1,
+    all2,
+    allw,
+    wide1,
+    wide2,
     in_sem,
     cot_sem,
     send_sem,
@@ -67,9 +74,12 @@
     mp = lax.axis_index("mp")
     ndev = ndp * nmp
     flat = dp * nmp + mp
+    half, side = lax.div(dp, 2), lax.rem(dp, 2)
     rows, ncols = master.shape
     parts = ncols // (SUB * LANES)
     deep = rows * SUB
+    high = parts * deep
+    lines = parts * SUB
     pieces = parts * loads_per_part
     width = ncols // pieces
 
@@ -87,9 +97,9 @@
                 (hidden_hbm, hidden),
                 (code1_hbm, code1),
                 (code2_hbm, code2),
-                (cols1_hbm, cols1),
-                (cols2_hbm, cols2),
                 (master_hbm, master),
+                (cols1_hbm, mcols.at[mp, pl.ds(0, lines)]),
+                (cols2_hbm, mcols.at[mp, pl.ds(lines, lines)]),
                 (rows1_hbm, rows1),
                 (rows2_hbm, rows2),
                 (step_hbm, step_count),
@@ -102,9 +112,26 @@
         )
         for c in range(pieces)
     ]
+
     def peer(k):
         other = lax.rem(flat + k + 1, ndev)
         return {"dp": lax.div(other, nmp), "mp": lax.rem(other, nmp)}
+
+    def send(src, dst, which, to):
+        pltpu.make_async_remote_copy(
+            src_ref=src,
+            dst_ref=dst,
+            send_sem=send_sem.at[which],
+            recv_sem=recv_sem.at[which],
+            device_id=to,
+            device_id_type=MESH,
+        ).start()
+
+    def dp_peer(k):
+        return {"dp": lax.rem(dp + k + 1, ndp)}
+
+    def mp_peer(k):
+        return {"mp": lax.rem(mp + k + 1, nmp)}
 
     barrier = pltpu.get_barrier_semaphore()
     loop(
@@ -123,14 +150,12 @@
     def send_share(p):
         def body(k):
             to = lax.rem(dp + k + 1, ndp)
-            pltpu.make_async_remote_copy(
-                src_ref=share.at[p, pl.ds(pl.multiple_of(to * deep, SUB), deep)],
-                dst_ref=grads.at[k, pl.ds(p * deep, deep)],
-                send_sem=send_sem.at[0],
-                recv_sem=recv_sem.at[0],
-                device_id={"dp": to},
-                device_id_type=MESH,
-            ).start()
+            send(
+                share.at[p, pl.ds(pl.multiple_of(to * deep, SUB), deep)],
+                grads.at[k, pl.ds(p * deep, deep)],
+                0,
+                {"dp": to},
+            )
 
         return body
 
@@ -162,6 +187,37 @@
     dense(code2[...].astype(F32), old2)
     dense(master[...], weights)
 
+    def quantize(x):
+        top = jnp.maximum(jnp.max(jnp.abs(x), axis=0, keepdims=True), 1e-30)
+        code = jnp.floor(x * (FULL / top) + 0.5)
+        return code.astype(jnp.int32).astype(I16), top * (1.0 / FULL)
+
+    lane = lax.broadcasted_iota(jnp.int32, (1, LANES), 1)
+    scales = jnp.zeros((1, LANES), F32)
+    for r in range(rows):
+        scales = jnp.where(lane == r, rows1[:, r : r + 1], scales)
+        scales = jnp.where(lane == rows + r, rows2[:, r : r + 1], scales)
+    coded, unit = quantize(weights[...])
+    pack = (old1[...] * 16.0 + old2[...]).astype(jnp.int32).astype(I16)
+    packs[half, side, 0:high] = pack
+    packs[half, side, high : 2 * high] = coded
+    mcodes[mp] = pack
+    metas[dp, 0:1] = scales
+    metas[dp, 1:2] = unit
+
+    loop(
+        ndp // 2 - 1,
+        lambda k: send(
+            packs.at[half, side],
+            packs.at[half, side],
+            2,
+            {"dp": lax.rem(dp + 2 * (k + 1), ndp)},
+        ),
+    )
+    loop(ndp - 1, lambda k: send(metas.at[dp], metas.at[dp], 4, dp_peer(k)))
+    loop(nmp - 1, lambda k: send(mcodes.at[mp], mcodes.at[mp], 5, mp_peer(k)))
+    loop(nmp - 1, lambda k: send(mcols.at[mp], mcols.at[mp], 6, mp_peer(k)))
+
     def scale(row_of, cols):
         tiles = []
         for p in range(parts):
@@ -173,10 +229,22 @@
         at = p * deep + r * SUB
         return x[at : at + SUB]
 
-    level1 = (old1[...] - 7.5) / 7.5
-    moment1 = 0.9 * (level1 * scale(lambda r: rows1[:, r : r + 1], cols1[...]))
-    level2 = (old2[...] + 1.0) / 16.0
-    moment2 = 0.95 * (level2 * level2 * scale(lambda r: rows2[:, r : r + 1], cols2[...]))
+    def first_of(code, row_of, cols):
+        return 0.9 * ((code - 7.5) / 7.5 * scale(row_of, cols))
+
+    def second_of(code, row_of, cols):
+        level = (code + 1.0) / 16.0
+        return 0.95 * (level * level * scale(row_of, cols))
+
+    def split(pack):
+        both = pack.astype(jnp.int32).astype(F32)
+        high_code = jnp.floor(both * 0.0625)
+        return high_code, both - 16.0 * high_code
+
+    cols1 = mcols[mp, 0:lines]
+    cols2 = mcols[mp, lines : 2 * lines]
+    moment1 = first_of(old1[...], lambda r: rows1[:, r : r + 1], cols1)
+    moment2 = second_of(old2[...], lambda r: rows2[:, r : r + 1], cols2)
     steps = step_count[...].astype(F32)
     fix1 = 1.0 - jnp.exp(steps * jnp.log(F32(0.9)))
     fix2 = 1.0 - jnp.exp(steps * jnp.log(F32(0.95)))
@@ -197,30 +265,71 @@
     wait_all(grads, ndp - 1, recv_sem.at[0])
     gradient = fold(jnp.add, gradient, grads, ndp - 1)
 
-    lanes = jnp.sum(gradient * gradient, axis=0, keepdims=True)
-    square[0] = lanes
-
-    def send_square(k):
-        pltpu.make_async_remote_copy(
-            src_ref=square.at[0],
-            dst_ref=squares.at[ndev - 2 - k],
-            send_sem=send_sem.at[1],
-            recv_sem=recv_sem.at[1],
-            device_id=peer(ndev - 2 - k),
-            device_id_type=MESH,
-        ).start()
-
-    loop(ndev - 1, send_square)
+    squares[flat] = jnp.sum(gradient * gradient, axis=0, keepdims=True)
+    loop(
+        ndev - 1,
+        lambda k: send(
+            squares.at[flat], squares.at[flat], 1, peer(ndev - 2 - k)
+        ),
+    )
+
+    coded, unit = quantize(gradient)
+    gq[dp] = coded
+    gm[mp] = coded
+    gscale[dp] = unit
+    gmscale[mp] = unit
+    loop(ndp - 1, lambda k: send(gq.at[dp], gq.at[dp], 7, dp_peer(k)))
+    loop(ndp - 1, lambda k: send(gscale.at[dp], gscale.at[dp], 8, dp_peer(k)))
+    loop(nmp - 1, lambda k: send(gm.at[mp], gm.at[mp], 9, mp_peer(k)))
+    loop(nmp - 1, lambda k: send(gmscale.at[mp], gmscale.at[mp], 10, mp_peer(k)))
+
+    column = packs.at[:, side]
+    others = column.at[pl.ds(0, ndp // 2 - 1)]
+    pltpu.make_async_copy(others, others, recv_sem.at[2]).wait()
+    send(column, column, 3, {"dp": dp + 1 - 2 * side})
+
+    wait_all(metas, ndp - 1, recv_sem.at[4])
+    wait_all(mcodes, nmp - 1, recv_sem.at[5])
+    wait_all(mcols, nmp - 1, recv_sem.at[6])
+
+    def prepare(j):
+        meta = metas[j]
+        code1, code2 = split(packs[j // 2, j % 2, 0:high])
+        all1[j] = first_of(code1, lambda r: meta[0:1, r : r + 1], cols1)
+        all2[j] = second_of(
+            code2, lambda r: meta[0:1, rows + r : rows + r + 1], cols2
+        )
+        known = packs[j // 2, j % 2, high : 2 * high]
+        allw[j] = known.astype(jnp.int32).astype(F32) * meta[1:2]
+
+    def prepare_wide(k):
+        code1, code2 = split(mcodes[k])
+        wide1[k] = first_of(code1, lambda r: rows1[:, r : r + 1], mcols[k, 0:lines])
+        wide2[k] = second_of(
+            code2, lambda r: rows2[:, r : r + 1], mcols[k, lines : 2 * lines]
+        )
+
+    loop(nmp, prepare_wide)
+    pltpu.make_async_copy(column, column, recv_sem.at[3]).wait()
+    if ndp <= 8:
+        for j in range(ndp):
+            prepare(j)
+    else:
+        lax.fori_loop(0, ndp, lambda j, c: (prepare(j), c)[1], 0)
+
     wait_all(squares, ndev - 1, recv_sem.at[1])
-    lanes = lanes + jnp.sum(squares[...], axis=0)
+    lanes = jnp.sum(squares[...], axis=0)
     norm = jnp.sqrt(jnp.sum(lanes, axis=1, keepdims=True))
     entries = rows * ncols * ndev
     clipf = jnp.minimum(1.0, 0.01 * jnp.sqrt(F32(entries)) / (norm + 1e-6))
+
     clipped = clipf * gradient
-
     new1 = moment1 + 0.1 * clipped
     new2 = moment2 + 0.05 * (clipped * clipped)
-    abs1 = jnp.abs(new1)
+    ratio = new1 / fix1 / (jnp.sqrt(new2 / fix2) + 1e-8)
+    old_weights = weights[...]
+    master_out[...] = old_weights - 0.001 * (ratio + 0.1 * old_weights)
+    ratio_out[...] = ratio
 
     def over_rows(x):
         tops = []
@@ -231,97 +340,75 @@
             tops.append(top)
         return jnp.concatenate(tops, axis=0)
 
-    maxcol[0, 0] = over_rows(abs1)
-    maxcol[0, 1] = over_rows(new2)
-
-    pair = pltpu.make_async_remote_copy(
-        src_ref=maxcol.at[0],
-        dst_ref=maxcol.at[1],
-        send_sem=send_sem.at[5],
-        recv_sem=recv_sem.at[5],
-        device_id={"dp": dp + 1 - 2 * lax.rem(dp, 2)},
-        device_id_type=MESH,
-    )
-    pair.start()
-
     def over_cols(x):
         tops = []
         for r in range(rows):
             top = tile(x, 0, r)
             for p in range(1, parts):
                 top = jnp.maximum(top, tile(x, p, r))
-            tops.append(jnp.max(top, axis=0, keepdims=True))
-        return tops
-
-    tops = jnp.concatenate(over_cols(abs1) + over_cols(new2), axis=0)
-    maxrow[0] = jnp.broadcast_to(jnp.max(tops, axis=1, keepdims=True), tops.shape)
-
-    def send_rows(k):
-        pltpu.make_async_remote_copy(
-            src_ref=maxrow.at[0],
-            dst_ref=maxrows.at[k],
-            send_sem=send_sem.at[3],
-            recv_sem=recv_sem.at[3],
-            device_id={"mp": lax.rem(mp + k + 1, nmp)},
-            device_id_type=MESH,
-        ).start()
-
-    loop(nmp - 1, send_rows)
-
-    ratio = new1 / fix1 / (jnp.sqrt(new2 / fix2) + 1e-8)
-    old_weights = weights[...]
-    new_weights = old_weights - 0.001 * (ratio + 0.1 * old_weights)
-    params[dp] = new_weights.astype(jnp.bfloat16)
-
-    def send_params(k):
-        pltpu.make_async_remote_copy(
-            src_ref=params.at[dp],
-            dst_ref=params.at[dp],
-            send_sem=send_sem.at[4],
-            recv_sem=recv_sem.at[4],
-            device_id={"dp": lax.rem(dp + k + 1, ndp)},
-            device_id_type=MESH,
-        ).start()
-
-    loop(ndp - 1, send_params)
-
-
-    def send_cols(k):
-        pltpu.make_async_remote_copy(
-            src_ref=maxcol.at[2],
-            dst_ref=maxcols.at[k],
-            send_sem=send_sem.at[2],
-            recv_sem=recv_sem.at[2],
-            device_id={"dp": lax.rem(dp + 2 * (k + 1), ndp)},
-            device_id_type=MESH,
-        ).start()
-
-    pair.wait_recv()
-    maxcol[2] = jnp.maximum(maxcol[0], maxcol[1])
-    loop(ndp // 2 - 1, send_cols)
-    master_out[...] = new_weights
-    ratio_out[...] = ratio
-
-    wait_all(maxrows, nmp - 1, recv_sem.at[3])
-    toprow = fold(jnp.maximum, maxrow[0], maxrows, nmp - 1)
+            tops.append(top)
+        return jnp.concatenate(tops, axis=0)
+
+    def renew(m1, m2, code, unit):
+        change = code.astype(jnp.int32).astype(F32) * (unit * clipf)
+        return m1 + 0.1 * change, m2 + 0.05 * (change * change)
+
+    wait_all(gm, nmp - 1, recv_sem.at[9])
+    wait_all(gmscale, nmp - 1, recv_sem.at[10])
+
+    def widen(k, tops):
+        now1, now2 = renew(wide1[k], wide2[k], gm[k], gmscale[k])
+        return (
+            jnp.maximum(tops[0], over_cols(jnp.abs(now1))),
+            jnp.maximum(tops[1], over_cols(now2)),
+        )
+
+    flat_top = jnp.zeros((deep, LANES), F32)
+    tops = lax.fori_loop(0, nmp, widen, (flat_top, flat_top), unroll=nmp <= 8)
+    toprow = jnp.concatenate(
+        [
+            jnp.max(x[r * SUB : (r + 1) * SUB], axis=0, keepdims=True)
+            for x in tops
+            for r in range(rows)
+        ],
+        axis=0,
+    )
+    toprow = jnp.broadcast_to(jnp.max(toprow, axis=1, keepdims=True), toprow.shape)
     rows_out[...] = toprow
-    wait_all(maxcols, ndp // 2 - 1, recv_sem.at[2])
-    topcol = fold(jnp.maximum, maxcol[2], maxcols, ndp // 2 - 1)
-    cols_out[...] = topcol
-    scaled1_out[...] = new1 / (scale(lambda r: toprow[r : r + 1], topcol[0]) + 1e-8)
+
+    wait_all(gq, ndp - 1, recv_sem.at[7])
+    wait_all(gscale, ndp - 1, recv_sem.at[8])
+
+    def finish(j, tops):
+        now1, now2 = renew(all1[j], all2[j], gq[j], gscale[j])
+        held = allw[j]
+        turn = now1 / fix1 / (jnp.sqrt(now2 / fix2) + 1e-8)
+        params_out[j] = (held - 0.001 * (turn + 0.1 * held)).astype(jnp.bfloat16)
+        return (
+            jnp.maximum(tops[0], over_rows(jnp.abs(now1))),
+            jnp.maximum(tops[1], over_rows(now2)),
+        )
+
+    flat_top = jnp.zeros((lines, LANES), F32)
+    top1, top2 = lax.fori_loop(0, ndp, finish, (flat_top, flat_top), unroll=ndp <= 8)
+    cols_out[0] = top1
+    cols_out[1] = top2
+    scaled1_out[...] = new1 / (scale(lambda r: toprow[r : r + 1], top1) + 1e-8)
     scaled2_out[...] = new2 / (
-        scale(lambda r: toprow[rows + r : rows + r + 1], topcol[1]) + 1e-8
-    )
-
-    wait_all(params, ndp - 1, recv_sem.at[4])
-    params_out[...] = params[...]
+        scale(lambda r: toprow[rows + r : rows + r + 1], top2) + 1e-8
+    )
 
     wait_all(grads, ndp - 1, send_sem.at[0])
     wait_all(squares, ndev - 1, send_sem.at[1])
-    pair.wait_send()
-    wait_all(maxcols, ndp // 2 - 1, send_sem.at[2])
-    wait_all(maxrows, nmp - 1, send_sem.at[3])
-    wait_all(params, ndp - 1, send_sem.at[4])
+    pltpu.make_async_copy(others, others, send_sem.at[2]).wait()
+    pltpu.make_async_copy(column, column, send_sem.at[3]).wait()
+    wait_all(metas, ndp - 1, send_sem.at[4])
+    wait_all(mcodes, nmp - 1, send_sem.at[5])
+    wait_all(mcols, nmp - 1, send_sem.at[6])
+    wait_all(gq, ndp - 1, send_sem.at[7])
+    wait_all(gscale, ndp - 1, send_sem.at[8])
+    wait_all(gm, nmp - 1, send_sem.at[9])
+    wait_all(gmscale, nmp - 1, send_sem.at[10])
 
 
 def unpack(
@@ -415,27 +502,32 @@
             pltpu.VMEM((rows, ncols), F32),
             pltpu.VMEM((rows, ncols), jnp.int32),
             pltpu.VMEM((rows, ncols), jnp.int32),
-            pltpu.VMEM(line, F32),
-            pltpu.VMEM(line, F32),
             pltpu.VMEM((1, rows), F32),
             pltpu.VMEM((1, rows), F32),
             pltpu.VMEM((1, 1), jnp.int32),
             pltpu.VMEM((parts, ndp * rows * SUB, LANES), F32),
             pltpu.VMEM((ndp - 1, *block), F32),
-            pltpu.VMEM((1, 1, LANES), F32),
-            pltpu.VMEM((ndp * nmp - 1, 1, LANES), F32),
-            pltpu.VMEM((ndp, *block), jnp.bfloat16),
-            pltpu.VMEM((3, 2, *line), F32),
-            pltpu.VMEM((ndp // 2 - 1, 2, *line), F32),
-            pltpu.VMEM((1, 2 * rows, LANES), F32),
-            pltpu.VMEM((nmp - 1, 2 * rows, LANES), F32),
+            pltpu.VMEM((ndp * nmp, 1, LANES), F32),
+            pltpu.VMEM((ndp // 2, 2, 2 * height, LANES), I16),
+            pltpu.VMEM((ndp, 2, LANES), F32),
+            pltpu.VMEM((nmp, *block), I16),
+            pltpu.VMEM((nmp, 2 * parts * SUB, LANES), F32),
+            pltpu.VMEM((ndp, *block), I16),
+            pltpu.VMEM((ndp, 1, LANES), F32),
+            pltpu.VMEM((nmp, *block), I16),
+            pltpu.VMEM((nmp, 1, LANES), F32),
             pltpu.VMEM(block, F32),
             pltpu.VMEM(block, F32),
             pltpu.VMEM(block, F32),
+            pltpu.VMEM((ndp, *block), F32),
+            pltpu.VMEM((ndp, *block), F32),
+            pltpu.VMEM((ndp, *block), F32),
+            pltpu.VMEM((nmp, *block), F32),
+            pltpu.VMEM((nmp, *block), F32),
             pltpu.SemaphoreType.DMA((9,)),
             pltpu.SemaphoreType.DMA((parts * loads,)),
-            pltpu.SemaphoreType.DMA((6,)),
-            pltpu.SemaphoreType.DMA((6,)),
+            pltpu.SemaphoreType.DMA((11,)),
+            pltpu.SemaphoreType.DMA((11,)),
         ],
         compiler_params=pltpu.CompilerParams(
             collective_id=0, has_side_effects=True, vmem_limit_bytes=60 * 1024 * 1024

time: 25.5 us -> 23 us (0.902)
  Pallas kernels: 24.1 us -> 21.5 us
    pallas_call x1, Pallas kernels: 23.3 us -> 20.8 us  [shards(): pl.pallas_call(functools.partial(kernel, ndp, nmp, loads), out_shape=(den...]
where the time goes in v1:
time: 23 us; the launch traced here: 22.8 us
  Pallas kernels  21.5 us (93%)
  between operations  1.3 us (6%)
    pallas_call x1, Pallas kernels, shards(): pl.pallas_call(functools.partial(kernel, ndp, nmp, loads), out_shape=(den...  20.8 us
    pallas_call x1, Pallas kernels, shards(): pl.pallas_call(unpack, out_shape=(whole, whole, jax.ShapeDtypeStruct((ndp...  0.76 us

profile of v1, /device:TPU:0, one launch (start us, length us, event | category | flops | bytes accessed | tf_op | source)
XLA Modules:
  0.0 22.8 jit_solution(14871653901807161727)
XLA Ops:
  1.3 20.8 %shard_map.169 = (f32[48,128]{1,0:T(8,128)S(1)}, f32[48,128]{1,0:T(8,128)S(1)}, bf16[8,48,128]{2,1,0:T(8,128)(2,1)S(1)}, f32[48,128]{1,0:T(8,128)S(1)}, f32[48,1...) custom-call(bf16[24,1024]{1,0:T(8,128)(2,1)} %bitcast.9, bf16[1024,2048]{1,0:T(8,128)(2,1)} %cot_hbm.1, ...), custom_call_target="tpu_custom_call" | custom-call | tf_op jit(solution)/shard_map/pallas_call | solution.py:486
  22.1 0.8 %shard_map.170 = (f32[3,2048]{1,0:T(4,128)}, f32[3,2048]{1,0:T(4,128)}, bf16[24,2048]{1,0:T(8,128)(2,1)}, f32[3,2048]{1,0:T(4,128)}, f32[3,2048]{1,0:T(4,128)}, ...) custom-call(f32[48,128]{1,0:T(8,128)S(1)} %get-tuple-element.25.master, ...), custom_call_target="tpu_custom_call" | custom-call | tf_op jit(solution)/shard_map/pallas_call | solution.py:549
